TPU v7x, 256 devices: a whole 4x4x8 slice. The times are simulated.
256 devices in a mesh: ta: 16 (over x, z_hi, core), gz: 4 (over y), gy: 4 (over z_lo).
Axes of the slice: x: 4, y: 4, z: 8 (z_hi: 2, z_lo: 4; z = z_hi * 4 + z_lo), core: 2. Of those that a mesh axis runs over, the one named last changes fastest.
Arguments:
- near_null: float32 [64, 16, 16, 12, 12, 128], P('ta', 'gz', 'gy'), may hold values from -400 to 400
- offsets: int32 [4], replicated, may hold values from 1 to 3
- owner_slot: int32 [16, 4, 4, 16], P('ta', 'gz', 'gy'), may hold values from 0 to 15, each once within a row
Outputs:
- result: float32 [4096, 2, 12, 6, 2, 256], P(('ta', 'gz', 'gy'))
Inputs may be any that keep to these rules, and one draw needn't show every extreme that they name: The same offsets hold for every device. `owner_slot`: each device's row is a permutation of 0 to 15.
All inputs are finite; a program needn't handle non-finite values.
Results may differ from a plain program's by a relative error of at most 0.0001.
Values sent between devices are 32-bit elements; how exact they have to be, the bound alone decides.
A program may use at most 256 MiB of HBM per device.

v0:
```python
import jax
import jax.numpy as jnp
from jax import lax
from jax.sharding import PartitionSpec as P

ridge_scale = 0.05
top_precision = lax.Precision.HIGHEST


def from_behind(array, axis, by):
    length = lax.axis_size(axis)
    return lax.ppermute(array, axis, [(i, (i + by) % length) for i in range(length)])


def factor_pass(blocks):
    norm_count = blocks.shape[3] * blocks.shape[5]
    products = (
        jnp.einsum("nkvcas,nkwcbs->nkavbw", blocks, blocks, precision=top_precision) / norm_count
    )
    gram_real = products[:, :, 0, :, 0, :] + products[:, :, 1, :, 1, :]
    gram_imag = products[:, :, 0, :, 1, :] - products[:, :, 1, :, 0, :]
    width = gram_real.shape[-1]
    diag_mean = jnp.mean(jnp.diagonal(gram_real, axis1=2, axis2=3), axis=-1)
    ridge_term = ridge_scale * (diag_mean + 1e-06)
    gram_real = jnp.moveaxis(gram_real, (2, 3), (0, 1))
    gram_imag = jnp.moveaxis(gram_imag, (2, 3), (0, 1))
    zero_batch = jnp.zeros_like(ridge_term)
    low_real = [[zero_batch] * width for row_idx in range(width)]
    low_imag = [[zero_batch] * width for row_idx in range(width)]
    for col_idx in range(width):
        remain = gram_real[col_idx, col_idx] + ridge_term
        for mid_idx in range(col_idx):
            remain = remain - low_real[col_idx][mid_idx] * low_real[col_idx][mid_idx]
            remain = remain - low_imag[col_idx][mid_idx] * low_imag[col_idx][mid_idx]
        diag_val = jnp.sqrt(remain)
        low_real[col_idx][col_idx] = diag_val
        for row_idx in range(col_idx + 1, width):
            sum_real = gram_real[row_idx, col_idx]
            sum_imag = gram_imag[row_idx, col_idx]
            for mid_idx in range(col_idx):
                left_real = low_real[row_idx][mid_idx]
                left_imag = low_imag[row_idx][mid_idx]
                right_real = low_real[col_idx][mid_idx]
                right_imag = low_imag[col_idx][mid_idx]
                sum_real = sum_real - (left_real * right_real + left_imag * right_imag)
                sum_imag = sum_imag - (left_imag * right_real - left_real * right_imag)
            low_real[row_idx][col_idx] = sum_real / diag_val
            low_imag[row_idx][col_idx] = sum_imag / diag_val
    inv_real = [[zero_batch] * width for row_idx in range(width)]
    inv_imag = [[zero_batch] * width for row_idx in range(width)]
    for col_idx in range(width):
        inv_real[col_idx][col_idx] = 1.0 / low_real[col_idx][col_idx]
        for row_idx in range(col_idx + 1, width):
            sum_real = zero_batch
            sum_imag = zero_batch
            for mid_idx in range(col_idx, row_idx):
                left_real = low_real[row_idx][mid_idx]
                left_imag = low_imag[row_idx][mid_idx]
                right_real = inv_real[mid_idx][col_idx]
                right_imag = inv_imag[mid_idx][col_idx]
                sum_real = sum_real + left_real * right_real - left_imag * right_imag
                sum_imag = sum_imag + left_real * right_imag + left_imag * right_real
            inv_real[row_idx][col_idx] = -sum_real / low_real[row_idx][row_idx]
            inv_imag[row_idx][col_idx] = -sum_imag / low_real[row_idx][row_idx]
    map_real = jnp.stack(
        [
            jnp.stack([inv_real[w_idx][v_idx] for w_idx in range(width)], axis=-1)
            for v_idx in range(width)
        ],
        axis=-2,
    )
    map_imag = -jnp.stack(
        [
            jnp.stack([inv_imag[w_idx][v_idx] for w_idx in range(width)], axis=-1)
            for v_idx in range(width)
        ],
        axis=-2,
    )
    mixing = jnp.stack(
        [jnp.stack([map_real, map_imag], axis=3), jnp.stack([-map_imag, map_real], axis=3)], axis=2
    )
    return jnp.einsum("nkvcas,nkavbw->nkwcbs", blocks, mixing, precision=top_precision)


def two_passes(blocks):
    return factor_pass(factor_pass(blocks))


def arrange(lattice, row_count, agg_edge):
    vector_count = lattice.shape[3]
    comp_count = lattice.shape[4]
    x_sites = lattice.shape[6]
    groups = x_sites // agg_edge
    pieces = lattice.reshape(
        row_count, agg_edge, agg_edge, vector_count, 2, comp_count // 2, 2, groups, agg_edge
    )
    pieces = pieces.transpose(7, 4, 3, 5, 6, 0, 1, 2, 8)
    return pieces.reshape(
        groups, 2, vector_count, comp_count // 2, 2, row_count * agg_edge * agg_edge * agg_edge
    )


def invert(slot_row):
    places = jnp.arange(slot_row.shape[0], dtype=jnp.int32)
    return jnp.sum(jnp.where(slot_row[None, :] == places[:, None], places[None, :], 0), axis=1)


def per_device(near_null, offsets, owner_slot):
    agg_edge = near_null.shape[0]
    rim_rows = agg_edge - 1
    from_z = from_behind(near_null[:, :rim_rows], "gz", -1)
    lattice = lax.dynamic_slice_in_dim(
        jnp.concatenate([near_null, from_z], axis=1), offsets[1], agg_edge, 1
    )
    from_y = from_behind(lattice[:, :, :rim_rows], "gy", -1)
    lattice = lax.dynamic_slice_in_dim(
        jnp.concatenate([lattice, from_y], axis=2), offsets[2], agg_edge, 2
    )
    x_sites = lattice.shape[5] // 2
    lattice = lattice.reshape(lattice.shape[:5] + (2, x_sites))
    lattice = lax.dynamic_slice_in_dim(
        jnp.concatenate([lattice, lattice], axis=6), offsets[3], x_sites, 6
    )
    slot_row = owner_slot.reshape(-1)
    source_of = invert(slot_row)
    from_t = from_behind(lattice[:rim_rows], "ta", -1)
    lattice = lax.dynamic_slice_in_dim(
        jnp.concatenate([lattice, from_t], axis=0), offsets[0], agg_edge, 0
    )
    tiles = arrange(lattice, agg_edge, agg_edge)
    packed = jnp.take(tiles, source_of, axis=0)
    result = two_passes(lax.all_to_all(packed, "ta", split_axis=0, concat_axis=0, tiled=True))
    return result


def solution(mesh):
    return jax.shard_map(
        per_device,
        mesh=mesh,
        in_specs=(P("ta", "gz", "gy", None, None, None), P(), P("ta", "gz", "gy", None)),
        out_specs=P(("ta", "gz", "gy"), None, None, None, None, None),
        check_vma=False,
    )
```

profile of v0, /device:TPU:1, one launch (start us, length us, event | category | flops | bytes accessed | tf_op | source)
XLA Modules:
  0.0 898.0 jit_solution(2452930418641187511)
XLA Ops:
  0.0 3.3 copy.21660
  3.3 2.7 copy-done.3
  6.0 2.5 slice.1218
  8.5 3.6 collective-permute-start
  12.0 0.7 fusion.1301
  14.6 98.2 %collective-permute-done = f32[4,3,4,12,12,128]{5,4,3,2,1,0:T(8,128)} collective-permute-done((f32[4,3,4,12,12,128]{5,4,3,2,1,0:T(8,128)}, f32[4,3,4,12,12,128]{5,4,3,2,1,0:T(8,128)}, u32[]{:S(2)}, u32[]{:S(2)}) %collective-permute-start) | collective-permute-done | bytes 3538976 | tf_op jit(solution)/shard_map/ppermute | solution.py:12
  112.8 4.2 fusion.2
  117.0 2.7 copy-done.2
  119.7 2.5 slice.1219
  122.2 4.3 collective-permute-start.1
  130.5 96.0 %collective-permute-done.1 = f32[4,4,3,12,12,128]{5,4,3,2,1,0:T(8,128)} collective-permute-done((f32[4,4,3,12,12,128]{5,4,3,2,1,0:T(8,128)}, f32[4,4,3,12,12,128]{5,4,3,2,1,0:T(8,128)}, u32[]{:S(2)}, u32[]{:S(2)}) %collective-permute-start.1) | collective-permute-done | bytes 3538976 | tf_op jit(solution)/shard_map/ppermute | solution.py:12
  226.5 7.5 fusion.1
  234.0 31.4 %copy.21661 = f32[4,4,4,12,12,128]{3,5,4,2,1,0:T(8,128)} copy(f32[4,4,4,12,12,128]{5,4,3,2,1,0:T(8,128)} %fusion.1) | data formatting | bytes 9437184 | tf_op jit(solution)/shard_map/dynamic_slice | solution.py:116
  265.3 32.4 %copy.21662 = f32[4,4,4,12,12,2,64]{6,2,5,4,3,1,0:T(4,128)} copy(f32[4,4,4,12,12,2,64]{3,6,5,4,2,1,0:T(8,128)} %bitcast.3155) | data formatting | bytes 9437184 | tf_op jit(solution)/shard_map/reshape | solution.py:120
  297.7 13.8 %dynamic-slice_maximum_fusion = f32[4,4,4,12,12,2,64]{6,2,5,4,3,1,0:T(4,128)S(1)} fusion(s32[]{:T(128)S(6)} %select_n.46, f32[4,4,4,12,12,2,64]{6,2,5,4,3,1,0:T(4,128)} %copy.21662), kind=kLoop, calls=%fused_computation.10 | loop fusion | flops 1179648 | bytes 9437188 | tf_op jit(solution)/shard_map/concatenate | solution.py:122
  311.5 5.9 slice.1220
  317.4 2.8 collective-permute-start.2
  322.3 123.4 %collective-permute-done.2 = f32[3,4,4,12,12,2,64]{6,2,5,4,3,1,0:T(4,128)} collective-permute-done((f32[3,4,4,12,12,2,64]{6,2,5,4,3,1,0:T(4,128)}, f32[3,4,4,12,12,2,64]{6,2,5,4,3,1,0:T(4,128)}, u32[]{:S(2)}, u32[]{:S(2)}) %collective-permute-start.2) | collective-permute-done | bytes 3538976 | tf_op jit(solution)/shard_map/ppermute | solution.py:12
  445.7 10.1 %fusion = f32[4,4,4,12,12,2,64]{6,2,5,4,3,1,0:T(4,128)} fusion(s32[]{:T(128)S(6)} %select_n.47, f32[4,4,4,12,12,2,64]{6,2,5,4,3,1,0:T(4,128)} %copy-done.1, f32[3,4,4,12,12,2,64]{6,2,5,4,3,1,0:T(4,128)} %collective-permute-done.2), kind=kLoop, calls=%fused_computation.9 | loop fusion | flops 1179648 | bytes 12976132 | tf_op jit(solution)/shard_map/concatenate | solution.py:128
  455.8 28.5 %copy.22101 = f32[4,4,4,12,12,2,64]{3,6,5,4,2,1,0:T(8,128)} copy(f32[4,4,4,12,12,2,64]{6,2,5,4,3,1,0:T(4,128)} %fusion) | data formatting | bytes 9437184
  484.3 70.6 %copy.21665 = f32[16,2,12,6,2,4,4,4,4]{0,8,7,6,5,4,3,2,1:T(4,128)} copy(f32[16,2,12,6,2,4,4,4,4]{2,8,0,4,3,1,7,6,5:T(4,128)} %bitcast.3156) | data formatting | bytes 9437184 | tf_op jit(solution)/shard_map/transpose | solution.py:97
  554.9 23.4 %copy.21666 = f32[16,2,12,6,2,256]{5,4,3,2,1,0:T(2,128)} copy(f32[16,2,12,6,2,256]{0,5,4,3,2,1:T(8,128)} %bitcast.3157) | data formatting | bytes 9437184 | tf_op jit(solution)/shard_map/reshape | solution.py:98
  578.3 9.3 %gather_fusion = f32[16,2,12,6,2,256]{5,4,3,2,1,0:T(2,128)} fusion(f32[16,2,12,6,2,256]{5,4,3,2,1,0:T(2,128)} %copy.21666, s32[1024]{0:T(1024)S(1)} %pad_clamp_fusion), kind=kCustom, calls=%fused_computation | custom fusion | bytes 9437248 | tf_op jit(solution)/shard_map/jit(_take)/gather | solution.py:131
  587.6 7.8 broadcast_select_fusion
  595.4 42.4 %all-to-all-start = ((f32[16,2,12,6,2,256]{5,4,3,2,1,0:T(2,128)}), f32[16,2,12,6,2,256]{5,4,3,2,1,0:T(2,128)}, u32[]{:S(2)}, u32[]{:S(2)}) async-start(f32[16,2,12,6,2,256]{5,4,3,2,1,0:T(2,128)} %broadcast_select_fusion), calls=%async_computation | async-start | bytes 9437184 | tf_op jit(solution)/shard_map/all_to_all | solution.py:132
  637.9 0.6 constant_dynamic-update-slice_fusion.237
  638.5 0.6 constant_dynamic-update-slice_fusion.327
  639.2 0.6 constant_dynamic-update-slice_fusion.215
  640.4 0.6 constant_dynamic-update-slice_fusion.326
  641.0 0.6 constant_dynamic-update-slice_fusion.236
  641.6 0.6 constant_dynamic-update-slice_fusion.246
  642.2 0.6 copy-done.13
  642.8 0.6 constant_dynamic-update-slice_fusion.276
  643.4 103.5 %all-to-all-done = f32[16,2,12,6,2,256]{5,4,3,2,1,0:T(2,128)} async-done(((f32[16,2,12,6,2,256]{5,4,3,2,1,0:T(2,128)}), f32[16,2,12,6,2,256]{5,4,3,2,1,0:T(2,128)}, u32[]{:S(2)}, u32[]{:S(2)}) %all-to-all-start) | async-done | bytes 4718624 | tf_op jit(solution)/shard_map/all_to_all | solution.py:132
  747.0 30.4 %fusion.31 = f32[16,2,2,12,2,12]{3,5,2,4,1,0:T(8,128)S(1)} fusion(f32[16,2,12,6,2,256,1]{5,4,3,2,1,0,6:T(2,128)} %bitcast.11), kind=kOutput, calls=%fused_computation.28 | convolution fusion | flops 339757056 | bytes 4792320 | tf_op jit(solution)/shard_map/nkvcas,nkwcbs->nkavbw/dot_general | solution.py:18
  777.6 0.7 fusion.1293
  778.3 0.7 fusion.1294
  779.0 0.7 fusion.1295
  779.7 0.7 fusion.1298
  780.8 0.7 fusion.1292
  781.5 0.7 fusion.1296
  782.2 0.7 fusion.1297
  796.5 0.7 gather_fusion.1
  805.9 1.0 copy.21844
  807.3 1.0 copy.21842
  808.7 1.0 copy.21840
  810.1 1.0 copy.21838
  811.2 2.4 stack.319
  813.6 1.0 neg.9834
  814.7 8.7 fusion.8
  823.4 26.3 %fusion.41 = f32[16,2,2,12,2,12]{3,5,2,4,1,0:T(8,128)S(1)} fusion(f32[16,2,2,12,6,256,1]{5,3,6,4,2,1,0:T(8,128)S(1)} %fusion.8), kind=kOutput, calls=%fused_computation.30 | convolution fusion | flops 339757056 | bytes 4792320 | tf_op jit(solution)/shard_map/nkvcas,nkwcbs->nkavbw/dot_general | solution.py:18
  849.9 0.7 fusion.1284
  850.6 0.7 fusion.1285
  851.3 0.7 fusion.1286
  852.0 0.7 fusion.1283
  852.8 0.7 fusion.1287
  853.5 0.7 fusion.1289
  854.2 0.7 fusion.1288
  867.9 0.7 gather_fusion.2
  879.5 1.0 copy.22010
  880.5 2.4 stack.386
  882.9 1.0 neg.9967
  884.0 7.9 fusion.13
  891.9 5.9 copy.22031
  (613 shorter events, 48.2 us)
Async XLA Ops:
  3.3 2.7 copy-start.3
  6.0 6.0 copy-start.23
  8.5 104.4 %collective-permute-start = (f32[4,3,4,12,12,128]{5,4,3,2,1,0:T(8,128)}, f32[4,3,4,12,12,128]{5,4,3,2,1,0:T(8,128)}, u32[]{:S(2)}, u32[]{:S(2)}) collective-permute-start(f32[4,3,4,12,12,128]{5,4,3,2,1,0:T(8,128)} %slice.1218), channel_id=1, source_target_pairs={{0,12},{4,0},{8,4},{12,8},{1,13},{5,1},{9,5},{13,9},{2,14},{6,2},{... | collective-permute-start | bytes 10616840 | tf_op jit(solution)/shard_map/ppermute | solution.py:12
  117.0 2.7 copy-start.2
  122.2 104.3 %collective-permute-start.1 = (f32[4,4,3,12,12,128]{5,4,3,2,1,0:T(8,128)}, f32[4,4,3,12,12,128]{5,4,3,2,1,0:T(8,128)}, u32[]{:S(2)}, u32[]{:S(2)}) collective-permute-start(f32[4,4,3,12,12,128]{5,4,3,2,1,0:T(8,128)} %slice.1219), channel_id=1, source_target_pairs={{0,3},{1,0},{2,1},{3,2},{4,7},{5,4},{6,5},{7,6},{8,11},{9,8},{10,9... | collective-permute-start | bytes 10616840 | tf_op jit(solution)/shard_map/ppermute | solution.py:12
  311.5 5.9 copy-start.1
  311.5 10.6 %copy-start.24 = (s32[1,1,1,16]{3,2,1,0:T(1,128)S(1)}, s32[1,1,1,16]{3,2,1,0:T(1,128)}, u32[]{:S(2)}) copy-start(s32[1,1,1,16]{3,2,1,0:T(1,128)} %param.5) | copy-start | bytes 196
  317.4 128.3 %collective-permute-start.2 = (f32[3,4,4,12,12,2,64]{6,2,5,4,3,1,0:T(4,128)}, f32[3,4,4,12,12,2,64]{6,2,5,4,3,1,0:T(4,128)}, u32[]{:S(2)}, u32[]{:S(2)}) collective-permute-start(f32[3,4,4,12,12,2,64]{6,2,5,4,3,1,0:T(4,128)} %slice.1220), channel_id=1, source_target_pairs={{0,240},{16,0},{32,16},{48,32},{64,48},{80,64},{96,80},{112,96},{1... | collective-permute-start | bytes 10616840 | tf_op jit(solution)/shard_map/ppermute | solution.py:12
  595.4 151.5 %all-to-all-start = ((f32[16,2,12,6,2,256]{5,4,3,2,1,0:T(2,128)}), f32[16,2,12,6,2,256]{5,4,3,2,1,0:T(2,128)}, u32[]{:S(2)}, u32[]{:S(2)}) async-start(f32[16,2,12,6,2,256]{5,4,3,2,1,0:T(2,128)} %broadcast_select_fusion), calls=%async_computation | async-start | bytes 9437184 | tf_op jit(solution)/shard_map/all_to_all | solution.py:132
  642.2 135.2 %copy-start.18 = (f32[16,2,12]{0,1,2:T(2,128)}, f32[16,2,12]{0,1,2:T(2,128)S(1)}, u32[]{:S(2)}) copy-start(f32[16,2,12]{0,1,2:T(2,128)S(1)} %get-tuple-element.1326) | copy-start | bytes 4612
  642.2 0.6 copy-start.13
  642.8 134.6 %copy-start.8 = (f32[16,2,12]{0,1,2:T(2,128)}, f32[16,2,12]{0,1,2:T(2,128)S(1)}, u32[]{:S(2)}) copy-start(f32[16,2,12]{0,1,2:T(2,128)S(1)} %get-tuple-element.1331) | copy-start | bytes 4612
  642.8 134.6 %copy-start.21 = (f32[16,2,12]{0,1,2:T(2,128)}, f32[16,2,12]{0,1,2:T(2,128)S(1)}, u32[]{:S(2)}) copy-start(f32[16,2,12]{0,1,2:T(2,128)S(1)} %get-tuple-element.1330) | copy-start | bytes 4612
  643.4 134.0 %copy-start.16 = (f32[16,2,12]{0,1,2:T(2,128)}, f32[16,2,12]{0,1,2:T(2,128)S(1)}, u32[]{:S(2)}) copy-start(f32[16,2,12]{0,1,2:T(2,128)S(1)} %get-tuple-element.1334) | copy-start | bytes 4612
  800.2 5.4 copy-start.5
  801.1 4.5 copy-start.4
  801.6 4.0 copy-start.6
  823.4 26.3 %copy-start = (f32[16,2,2,12,6,256,1]{5,3,6,4,2,1,0:T(8,128)}, f32[16,2,2,12,6,256,1]{5,3,6,4,2,1,0:T(8,128)S(1)}, u32[]{:S(2)}) copy-start(f32[16,2,2,12,6,256,1]{5,3,6,4,2,1,0:T(8,128)S(1)} %fusion.8) | copy-start | bytes 14155780
  849.7 20.4 %copy-start.12 = (f32[16,2,12]{0,1,2:T(2,128)S(1)}, f32[16,2,12]{0,1,2:T(2,128)}, u32[]{:S(2)}) copy-start(f32[16,2,12]{0,1,2:T(2,128)} %constant_dynamic-update-slice_fusion.226) | copy-start | bytes 4612
  849.7 20.5 %copy-start.15 = (f32[16,2,12]{0,1,2:T(2,128)S(1)}, f32[16,2,12]{0,1,2:T(2,128)}, u32[]{:S(2)}) copy-start(f32[16,2,12]{0,1,2:T(2,128)} %get-tuple-element.1320) | copy-start | bytes 4612
  849.7 20.5 %copy-start.7 = (f32[16,2,12]{0,1,2:T(2,128)S(1)}, f32[16,2,12]{0,1,2:T(2,128)}, u32[]{:S(2)}) copy-start(f32[16,2,12]{0,1,2:T(2,128)} %constant_dynamic-update-slice_fusion.326) | copy-start | bytes 4612
  849.7 20.5 %copy-start.20 = (f32[16,2,12]{0,1,2:T(2,128)S(1)}, f32[16,2,12]{0,1,2:T(2,128)}, u32[]{:S(2)}) copy-start(f32[16,2,12]{0,1,2:T(2,128)} %get-tuple-element.1322) | copy-start | bytes 4612
  849.7 20.6 %copy-start.11 = (f32[16,2,12]{0,1,2:T(2,128)S(1)}, f32[16,2,12]{0,1,2:T(2,128)}, u32[]{:S(2)}) copy-start(f32[16,2,12]{0,1,2:T(2,128)} %get-tuple-element.1324) | copy-start | bytes 4612
  849.7 20.8 %copy-start.19 = (f32[16,2,12]{0,1,2:T(2,128)S(1)}, f32[16,2,12]{0,1,2:T(2,128)}, u32[]{:S(2)}) copy-start(f32[16,2,12]{0,1,2:T(2,128)} %copy-done.18) | copy-start | bytes 4612
  849.8 21.1 %copy-start.14 = (f32[16,2,12]{0,1,2:T(2,128)S(1)}, f32[16,2,12]{0,1,2:T(2,128)}, u32[]{:S(2)}) copy-start(f32[16,2,12]{0,1,2:T(2,128)} %copy-done.13) | copy-start | bytes 4612
  849.8 21.5 %copy-start.9 = (f32[16,2,12]{0,1,2:T(2,128)S(1)}, f32[16,2,12]{0,1,2:T(2,128)}, u32[]{:S(2)}) copy-start(f32[16,2,12]{0,1,2:T(2,128)} %copy-done.8) | copy-start | bytes 4612
  849.8 21.5 %copy-start.22 = (f32[16,2,12]{0,1,2:T(2,128)S(1)}, f32[16,2,12]{0,1,2:T(2,128)}, u32[]{:S(2)}) copy-start(f32[16,2,12]{0,1,2:T(2,128)} %copy-done.21) | copy-start | bytes 4612
  849.8 22.0 %copy-start.10 = (f32[16,2,12]{0,1,2:T(2,128)S(1)}, f32[16,2,12]{0,1,2:T(2,128)}, u32[]{:S(2)}) copy-start(f32[16,2,12]{0,1,2:T(2,128)} %get-tuple-element.1332) | copy-start | bytes 4612
  849.8 22.5 %copy-start.17 = (f32[16,2,12]{0,1,2:T(2,128)S(1)}, f32[16,2,12]{0,1,2:T(2,128)}, u32[]{:S(2)}) copy-start(f32[16,2,12]{0,1,2:T(2,128)} %copy-done.16) | copy-start | bytes 4612
where the time goes:
time: 911 us; the launch traced here: 898 us
  waiting for transfers between devices  421 us (46%)
  local copies, waits for them, and re-layouts  285 us (31%)
  matrix products  73.3 us (8%)
  other arithmetic  56.1 us (6%)
  starting transfers between devices  53.1 us (6%)
  between operations  9.27 us (1%)
    ppermute x3, waiting for transfers between devices, from_behind(): lax.ppermute(array, axis, [(i, (i + by) % length) for i in range(length)])  318 us
    all_to_all x1, waiting for transfers between devices, per_device(): lax.all_to_all(packed, 'ta', split_axis=0, concat_axis=0, tiled=True)  104 us
    transpose x1, local copies, waits for them, and re-layouts, arrange(): pieces = pieces.transpose(7, 4, 3, 5, 6, 0, 1, 2, 8)  70.6 us
    dot_general x2, matrix products, factor_pass(): jnp.einsum('nkvcas,nkwcbs->nkavbw', blocks, blocks, precision=top_precision)  56.7 us
    unnamed x137, local copies, waits for them, and re-layouts  42.9 us
    all_to_all x1, starting transfers between devices, per_device(): lax.all_to_all(packed, 'ta', split_axis=0, concat_axis=0, tiled=True)  42.4 us
    reshape x1, local copies, waits for them, and re-layouts, per_device(): lattice = lattice.reshape(lattice.shape[:5] + (2, x_sites))  32.4 us
    dynamic_slice x1, local copies, waits for them, and re-layouts, per_device(): lax.dynamic_slice_in_dim(jnp.concatenate([lattice, from_y], axis=2), offs...  31.4 us
  transfers between devices with their start and end apart: 4, of which 4 were waited for; matrix products, arithmetic and copies ran while one was open for 1% of the time, Pallas kernels for 0%

commit v1 on v0

v1 whole, which is shorter than its diff:
```python
import functools

import jax
import jax.numpy as jnp
from jax import lax
from jax.experimental import pallas as pl
from jax.experimental.pallas import tpu as pltpu
from jax.sharding import PartitionSpec as P

MESH = pl.DeviceIdType.MESH

HIGH = lax.Precision.HIGHEST
RIDGE = 0.05


def swap_bits(arrays, bit, distance):
    lanes = lax.broadcasted_iota(jnp.int32, arrays[0].shape, 1)
    low = (lanes & distance) == 0
    out = list(arrays)
    for first in range(len(arrays)):
        if first & (1 << bit):
            continue
        second = first | (1 << bit)
        a, b = arrays[first], arrays[second]
        out[first] = jnp.where(low, a, pltpu.roll(b, distance, 1))
        out[second] = jnp.where(low, pltpu.roll(a, 128 - distance, 1), b)
    return out


def pack_kernel(off_ref, slot_ref, x_ref, s_ref, tiles, place):
    cell_z, cell_y = pl.program_id(0), pl.program_id(1)
    ot, oz, oy, ox = off_ref[0], off_ref[1], off_ref[2], off_ref[3]

    @pl.when((cell_z == 0) & (cell_y == 0))
    def _():
        def fill(i, _):
            place[i // 16, slot_ref[i // 16, i % 16]] = i % 16
            return 0
        lax.fori_loop(0, 128, fill, 0)

    lanes = lax.broadcasted_iota(jnp.int32, (12, 128), 1)
    inside = (lanes & 63) < 64 - ox
    for vb in range(3):
        arrays = []
        for t in range(4):
            for m in range(4):
                row = x_ref[(t + ot) & 3, 0, 0, 4 * vb + m]
                turned = pltpu.roll(row, 128 - ox, 1)
                arrays.append(jnp.where(inside, turned, pltpu.roll(turned, 64, 1)))
        for bit in range(4):
            arrays = swap_bits(arrays, bit, 4 << bit)
        for j in range(16):
            for part in range(3):
                tiles[j, 3 * vb + part] = arrays[j][4 * part:4 * part + 4]
    home = 2 * (cell_z >= 4 - oz).astype(jnp.int32) + (cell_y >= 4 - oy).astype(jnp.int32)
    lane3 = lax.broadcasted_iota(jnp.int32, (9, 4, 128), 2)
    mine = ((lane3 >> 4) & 3) < 4 - ot
    def emit(q, _):
        s_ref[q, 0, 0] = jnp.where(mine, tiles[place[home, q]], tiles[place[4 + home, q]])
        return 0
    lax.fori_loop(0, 16, emit, 0)


def pack(offsets, slots, x):
    def at(z, y, off, slot):
        return (0, (z + off[1]) & 3, (y + off[2]) & 3, 0, 0, 0)
    return pl.pallas_call(
        pack_kernel,
        out_shape=jax.ShapeDtypeStruct((16, 4, 4, 9, 4, 128), jnp.float32),
        grid_spec=pltpu.PrefetchScalarGridSpec(
            num_scalar_prefetch=2,
            grid=(4, 4),
            in_specs=[pl.BlockSpec((4, 1, 1, 12, 12, 128), at)],
            out_specs=pl.BlockSpec((16, 1, 1, 9, 4, 128), lambda z, y, off, slot: (0, z, y, 0, 0, 0)),
            scratch_shapes=[pltpu.VMEM((16, 9, 4, 128), jnp.float32), pltpu.SMEM((8, 16), jnp.int32)],
        ),
        compiler_params=pltpu.CompilerParams(dimension_semantics=("arbitrary", "arbitrary")),
        name="pack",
    )(offsets, slots, x)


def cmul_sub(ar, ai, br, bi, cr, ci):
    return ar - (br * cr - bi * ci), ai - (br * ci + bi * cr)


def factor(gr, gi, rows):
    gr, gi = list(gr), list(gi)
    diag = gr[0][0:1]
    for v in range(1, 12):
        diag = diag + gr[v][v:v + 1]
    ridge = RIDGE * (diag / 12.0 + 1e-06)
    low_r, low_i, inv = [None] * 12, [None] * 12, [None] * 12
    for j in range(12):
        d = jnp.sqrt(gr[j][j:j + 1] + ridge)
        inv[j] = 1.0 / d
        below = rows > j
        low_r[j] = jnp.where(below, gr[j] * inv[j], 0.0)
        low_i[j] = jnp.where(below, gi[j] * inv[j], 0.0)
        for w in range(j + 1, 12):
            wr, wi = low_r[j][w:w + 1], low_i[j][w:w + 1]
            gr[w] = gr[w] - (low_r[j] * wr + low_i[j] * wi)
            gi[w] = gi[w] - (low_i[j] * wr - low_r[j] * wi)
    xr, xi = [], []
    for c in range(12):
        ar = jnp.where(rows == c, inv[c], 0.0)
        ai = jnp.zeros_like(ar)
        for m in range(c, 12):
            if m > c:
                here = rows == m
                ar = jnp.where(here, ar * inv[m], ar)
                ai = jnp.where(here, ai * inv[m], ai)
            if m < 11:
                ar, ai = cmul_sub(ar, ai, low_r[m], low_i[m], ar[m:m + 1], ai[m:m + 1])
        xr.append(ar)
        xi.append(ai)
    return xr, xi


def small_product(ar, ai, entry, span):
    out_r, out_i = [], []
    for c in range(12):
        sr = si = None
        for l in span(c):
            er, ei = entry(l, c)
            tr = ar[l] * er - ai[l] * ei
            ti = ar[l] * ei + ai[l] * er
            sr, si = (tr, ti) if sr is None else (sr + tr, si + ti)
        out_r.append(sr)
        out_i.append(si)
    return out_r, out_i


def finish_kernel(off_ref, r_ref, o_ref, sites, grams, maps):
    ot = off_ref[0]
    lanes = lax.broadcasted_iota(jnp.int32, (12, 128), 1)
    mine = ((lanes >> 4) & 3) < 4 - ot

    def unpack(n, _):
        after = (n + 1) & 15
        for vb in range(3):
            arrays = []
            for cell in range(16):
                rows = pl.ds(cell * 36 + vb * 12, 12)
                arrays.append(jnp.where(mine, r_ref[n, rows], r_ref[after, rows]))
            for bit in range(4):
                arrays = swap_bits(arrays, bit, 4 << bit)
            arrays = swap_bits(arrays, 2, 64)
            for at in range(16):
                thi, ri, m = at >> 3, (at >> 2) & 1, at & 3
                sites[n, thi, pl.ds(ri * 12 + 4 * vb + m, 12, stride=24)] = arrays[at]
        return 0
    lax.fori_loop(0, 16, unpack, 0)

    def operand(group, c):
        parts = [sites[pl.ds(4 * group, 4), thi, pl.ds(c * 24, 24)].reshape(96, 128) for thi in range(2)]
        return jnp.concatenate(parts, axis=1)

    def gram(step, _):
        h, group = step // 4, step % 4
        def add(k, total):
            block = operand(group, h * 6 + k)
            return total + lax.dot_general(block, block, (((1,), (1,)), ((), ())), precision=HIGH, preferred_element_type=jnp.float32)
        total = lax.fori_loop(0, 6, add, jnp.zeros((96, 96), jnp.float32)) / 1536.0
        total = jnp.concatenate([total, jnp.zeros((96, 32), jnp.float32)], axis=1)
        for i in range(4):
            piece = total[24 * i:24 * i + 24]
            if i:
                piece = pltpu.roll(piece, 128 - 24 * i, 1)
            grams[pl.ds((h * 16 + group * 4 + i) * 24, 24)] = piece
        return 0
    lax.fori_loop(0, 8, gram, 0)

    lane128 = lax.broadcasted_iota(jnp.int32, (24, 128), 1)
    columns = []
    for four in range(6):
        stack = jnp.concatenate([grams[pl.ds(4 * four + i, 32, stride=24)] for i in range(4)], axis=0)
        turned = jnp.transpose(stack)[0:24]
        for i in range(4):
            columns.append(pltpu.roll(turned, 128 - 32 * i, 1) if i else turned)
    columns = [jnp.where(lane128 < 32, column, 0.0) for column in columns]
    rows = lax.broadcasted_iota(jnp.int32, (12, 128), 0)
    gr = [columns[w][0:12] + columns[12 + w][12:24] for w in range(12)]
    gi = [columns[12 + w][0:12] - columns[w][12:24] for w in range(12)]
    xr, xi = factor(gr, gi, rows)
    tr, ti = small_product(xr, xi, lambda l, c: (gr[c][l:l + 1], gi[c][l:l + 1]), lambda c: range(12))
    sr, si = small_product(tr, ti, lambda l, c: (xr[l][c:c + 1], -xi[l][c:c + 1]), lambda c: range(c + 1))
    yr, yi = factor(sr, si, rows)
    mr, mi = small_product(yr, yi, lambda l, c: (xr[c][l:l + 1], xi[c][l:l + 1]), lambda c: range(c, 12))

    for four in range(6):
        stack = None
        for i in range(4):
            r = 4 * four + i
            v = r % 12
            column = jnp.concatenate([mr[v], -mi[v]] if r < 12 else [mi[v], mr[v]], axis=0)
            column = jnp.where(lane128 < 32, column, 0.0)
            if i:
                column = pltpu.roll(column, 32 * i, 1)
            stack = column if stack is None else stack + column
        stack = jnp.concatenate([stack, jnp.zeros((104, 128), jnp.float32)], axis=0)
        turned = jnp.transpose(stack)
        for i in range(4):
            maps[pl.ds(4 * four + i, 32, stride=24)] = turned[32 * i:32 * i + 32]

    def apply(step, _):
        h, group = step // 4, step % 4
        parts = []
        for i in range(4):
            piece = maps[pl.ds((h * 16 + group * 4 + i) * 24, 24)]
            parts.append(pltpu.roll(piece, 24 * i, 1) if i else piece)
        parts.append(jnp.zeros((32, 128), jnp.float32))
        mixing = jnp.transpose(jnp.concatenate(parts, axis=0))[0:96, 0:96]
        def one(k, _):
            block = operand(group, h * 6 + k)
            out = lax.dot_general(mixing, block, (((1,), (0,)), ((), ())), precision=HIGH, preferred_element_type=jnp.float32)
            for i in range(4):
                for ri in range(2):
                    for col in range(2):
                        start = (((group * 4 + i) * 2 + h) * 12) * 24 + k * 4 + col * 2 + ri
                        o_ref[pl.ds(start, 12, stride=24)] = out[24 * i + 12 * ri:24 * i + 12 * ri + 12, 128 * col:128 * col + 128]
            return 0
        lax.fori_loop(0, 6, one, 0)
        return 0
    lax.fori_loop(0, 8, apply, 0)


def finish(offsets, r):
    out = pl.pallas_call(
        finish_kernel,
        out_shape=jax.ShapeDtypeStruct((9216, 128), jnp.float32),
        in_specs=[pl.BlockSpec(memory_space=pltpu.SMEM), pl.BlockSpec(memory_space=pltpu.VMEM)],
        out_specs=pl.BlockSpec(memory_space=pltpu.VMEM),
        scratch_shapes=[
            pltpu.VMEM((16, 2, 288, 128), jnp.float32),
            pltpu.VMEM((768, 128), jnp.float32),
            pltpu.VMEM((768, 128), jnp.float32),
        ],
        name="finish",
    )(offsets, r.reshape(16, 576, 128))
    out = out.reshape(16, 2, 12, 6, 2, 2, 128)
    return out.transpose(0, 1, 2, 3, 5, 4, 6).reshape(16, 2, 12, 6, 2, 256)


WAYS = ((1, 1), (1, 0), (0, 1), (0, 0))


def exchange_kernel(oz, oy, s_ref, r_ref, send, recv, local):
    a, b, c = lax.axis_index("ta"), lax.axis_index("gz"), lax.axis_index("gy")
    n_a, n_b, n_c = lax.axis_size("ta"), lax.axis_size("gz"), lax.axis_size("gy")
    spans_z = ((0, 4 - oz), (4 - oz, oz))
    spans_y = ((0, 4 - oy), (4 - oy, oy))

    barrier = pltpu.get_barrier_semaphore()

    def greet(step, _):
        q = lax.rem(a + step, n_a)
        for dz, dy in WAYS[:3]:
            peer = (q, lax.rem(b + dz, n_b), lax.rem(c + dy, n_c))
            pl.semaphore_signal(barrier, inc=1, device_id=peer, device_id_type=MESH)

        @pl.when(step < n_a)
        def _():
            pl.semaphore_signal(barrier, inc=1, device_id=(q, b, c), device_id_type=MESH)

        return 0

    lax.fori_loop(1, n_a + 1, greet, 0)
    pl.semaphore_wait(barrier, 4 * n_a - 1)

    def view(ref, at, dz, dy):
        z0, nz = spans_z[dz]
        y0, ny = spans_y[dy]
        return ref.at[at, pl.ds(z0, nz), pl.ds(y0, ny)]

    def copy(way, q, lands):
        dz, dy = WAYS[way]
        return pltpu.make_async_remote_copy(
            view(s_ref, q, dz, dy),
            view(r_ref, lands, dz, dy),
            send.at[way, q],
            recv.at[way, lands],
            device_id=(q, lax.rem(b + n_b - dz, n_b), lax.rem(c + n_c - dy, n_c)),
            device_id_type=MESH,
        )

    def start(step, _):
        q = lax.rem(a + step, n_a)
        for way in range(3):
            copy(way, q, a).start()
        pl.when(step < n_a)(copy(3, q, a).start)
        return 0

    own = pltpu.make_async_copy(view(s_ref, a, 0, 0), view(r_ref, a, 0, 0), local)
    lax.fori_loop(1, n_a + 1, start, 0)
    own.start()

    def finish_one(way, q):
        one = copy(way, q, q)
        one.wait_send()
        one.wait_recv()

    def wait(step, _):
        q = lax.rem(a + step, n_a)
        for way in range(3):
            finish_one(way, q)
        pl.when(step < n_a)(functools.partial(finish_one, 3, q))
        return 0

    lax.fori_loop(1, n_a + 1, wait, 0)
    own.wait()


def exchange(s, oz, oy):
    return pl.pallas_call(
        functools.partial(exchange_kernel, oz, oy),
        out_shape=jax.ShapeDtypeStruct(s.shape, s.dtype),
        in_specs=[pl.BlockSpec(memory_space=pl.ANY)],
        out_specs=pl.BlockSpec(memory_space=pl.ANY),
        scratch_shapes=[pltpu.SemaphoreType.DMA((4, 16)), pltpu.SemaphoreType.DMA((4, 16)), pltpu.SemaphoreType.DMA],
        compiler_params=pltpu.CompilerParams(has_side_effects=True, collective_id=3 * (oz - 1) + oy - 1),
        name=f"exchange_{oz}{oy}",
    )(s)


def ahead(array, axis):
    length = lax.axis_size(axis)
    return lax.ppermute(array, axis, [(i, (i + 1) % length) for i in range(length)])


def per_device(near_null, offsets, owner_slot):
    slots = owner_slot.reshape(1, 16)
    for axis in ("gy", "gz", "ta"):
        slots = jnp.concatenate([slots, ahead(slots, axis)], axis=0)
    s = pack(offsets, slots, near_null)
    branches = [functools.partial(exchange, oz=oz, oy=oy) for oz in (1, 2, 3) for oy in (1, 2, 3)]
    r = lax.switch(3 * (offsets[1] - 1) + offsets[2] - 1, branches, s)
    return finish(offsets, r)


def solution(mesh):
    return jax.shard_map(
        per_device,
        mesh=mesh,
        in_specs=(P("ta", "gz", "gy", None, None, None), P(), P("ta", "gz", "gy", None)),
        out_specs=P(("ta", "gz", "gy"), None, None, None, None, None),
        check_vma=False,
    )
```

time: 911 us -> 244 us (0.27); the launches traced: 898 us -> 244 us
  waiting for transfers between devices: 421 us -> 3.67 us
  local copies, waits for them, and re-layouts: 285 us -> 7.25 us
  Pallas kernels: 0 us -> 217 us
  matrix products: 73.3 us -> 0 us
  other arithmetic: 56.1 us -> 1.93 us
  starting transfers between devices: 53.1 us -> 12.5 us
    ppermute x3, waiting for transfers between devices: 318 us -> 3.67 us  [ahead(): lax.ppermute(array, axis, [(i, (i + 1) % length) for i in range(length)])]
    pallas_call x0 -> x3, Pallas kernels: none -> 217 us  [the longest x1 130 us: exchange(): pl.pallas_call(functools.partial(exchange_kernel, oz, oy), out_shape=jax....]
    all_to_all x1 -> x0, waiting for transfers between devices: 104 us -> none  [per_device(): lax.all_to_all(packed, 'ta', split_axis=0, concat_axis=0, tiled=True)]
    transpose x2 -> x0, local copies, waits for them, and re-layouts: 76.5 us -> none  [the longest x1 70.6 us: arrange(): pieces = pieces.transpose(7, 4, 3, 5, 6, 0, 1, 2, 8)]
    dot_general x4 -> x0, matrix products: 73.3 us -> none  [the longest x2 56.7 us: factor_pass(): jnp.einsum('nkvcas,nkwcbs->nkavbw', blocks, blocks, precision=top_precision)]
    reshape x2 -> x0, local copies, waits for them, and re-layouts: 55.7 us -> none  [the longest x1 32.4 us: per_device(): lattice = lattice.reshape(lattice.shape[:5] + (2, x_sites))]
    slice x309 -> x1, local copies, waits for them, and re-layouts: 48.6 us -> 1.31 us  [per_device(): r = lax.switch(3 * (offsets[1] - 1) + offsets[2] - 1, branches, s)]
    all_to_all x1 -> x0, starting transfers between devices: 42.4 us -> none  [per_device(): lax.all_to_all(packed, 'ta', split_axis=0, concat_axis=0, tiled=True)]
  transfers between devices with their start and end apart: 4 -> 3, of which waited for: 4 -> 2; matrix products, arithmetic and copies ran while one was open for 1% -> 3% of each run, Pallas kernels for 0% -> 0%
where the time goes in v1:
time: 244 us
  Pallas kernels  217 us (89%)
  starting transfers between devices  12.5 us (5%)
  local copies, waits for them, and re-layouts  7.25 us (3%)
  waiting for transfers between devices  3.67 us (2%)
    pallas_call x1, Pallas kernels, exchange(): pl.pallas_call(functools.partial(exchange_kernel, oz, oy), out_shape=jax....  130 us
    pallas_call x1, Pallas kernels, finish(): pl.pallas_call(finish_kernel, out_shape=jax.ShapeDtypeStruct((9216, 128),...  46.9 us
    pallas_call x1, Pallas kernels, pack(): pl.pallas_call(pack_kernel, out_shape=jax.ShapeDtypeStruct((16, 4, 4, 9,...  40.7 us
    ppermute x3, starting transfers between devices, ahead(): lax.ppermute(array, axis, [(i, (i + 1) % length) for i in range(length)])  12.5 us
    unnamed x3, local copies, waits for them, and re-layouts  5.94 us
  transfers between devices with their start and end apart: 3, of which 2 were waited for; matrix products, arithmetic and copies ran while one was open for 3% of the time, Pallas kernels for 0%

profile of v1, /device:TPU:1, one launch (start us, length us, event | category | flops | bytes accessed | tf_op | source)
XLA Modules:
  0.0 243.7 jit_solution(14612277249039581246)
XLA Ops:
  0.0 2.5 %collective-permute-start = (s32[1,16]{1,0:T(1,128)}, s32[1,16]{1,0:T(1,128)S(1)}, u32[]{:S(2)}, u32[]{:S(2)}) collective-permute-start(s32[1,16]{1,0:T(1,128)} %bitcast.25), channel_id=1, source_target_pairs={{0,1},{1,2},{2,3},{3,0},{4,5},{5,6},{6,7},{7,4},{8,9},{9,10},{10,1... | collective-permute-start | bytes 200 | tf_op jit(solution)/shard_map/ppermute | solution.py:327
  2.5 1.3 fusion
  4.3 1.9 collective-permute-done
  6.3 0.7 pad_add_fusion.2
  6.9 1.3 collective-permute-start.1
  8.9 1.7 collective-permute-done.1
  10.6 0.7 pad_add_fusion.1
  11.3 0.0 copy-start
  11.3 8.7 %collective-permute-start.2 = (s32[4,16]{1,0:T(4,128)S(1)}, s32[4,16]{1,0:T(4,128)S(1)}, u32[]{:S(2)}, u32[]{:S(2)}) collective-permute-start(s32[4,16]{1,0:T(4,128)S(1)} %pad_add_fusion.1), channel_id=1, source_target_pairs={{0,16},{16,32},{32,48},{48,64},{64,80},{80,96},{96,112},{112,128},... | collective-permute-start | bytes 776 | tf_op jit(solution)/shard_map/ppermute | solution.py:327
  20.0 5.9 %copy.4.x_ref = f32[4,4,4,12,12,128]{5,4,3,2,1,0:T(8,128)} copy(f32[4,4,4,12,12,128]{5,2,4,3,1,0:T(4,128)} %param.12) | data formatting | bytes 9437184 | tf_op args[0]
  25.9 0.0 collective-permute-done.2
  25.9 0.0 copy-done
  25.9 0.6 pad_add_fusion.slot_ref
  26.5 40.7 %pack.1 = f32[16,4,4,9,4,128]{5,4,3,2,1,0:T(4,128)} custom-call(s32[4]{0:T(128)} %off_ref.3, s32[8,16]{1,0:T(8,128)} %pad_add_fusion.slot_ref, f32[4,4,4,12,12,128]{5,4,3,2,1,0:T(8,128)} %copy.4.x_ref), custom_call_target="tpu_custom_call" | custom-call | tf_op jit(solution)/shard_map/pack/pallas_call | solution.py:67
  67.3 129.5 %conditional.1 = (f32[16,576,128]{2,1,0:T(8,128)}) conditional(s32[]{:T(128)} %bitcast.9, f32[16,4,4,9,4,128]{5,4,3,2,1,0:T(4,128)} %pack.1, f32[16,4,4,9,4,128]{5,4,3,2,1,0:T(4,128)} %pack.1, f32[16,4,4,9,4,128]{5,4,3,2,1,0:T(4,128)} %pack.1, f32[16,4,4,9,4,128]{5,4,3,2,1,0:T(4,128)} %pack.1, ...), branch_computations={%region_0.0_spmd, %region_1.0_spmd, %region_2.0_spmd, %region_3.0_... | conditional | bytes 8 | solution.py:336
  67.3 129.5 %exchange_31.1 = f32[16,4,4,9,4,128]{5,4,3,2,1,0:T(4,128)} custom-call(f32[16,4,4,9,4,128]{5,4,3,2,1,0:T(4,128)} %s_ref.6), custom_call_target="tpu_custom_call" | custom-call | tf_op jit(solution)/shard_map/cond/branch_6_fun/exchange_31/pallas_call | solution.py:314
  196.8 46.9 %finish.1 = f32[9216,128]{1,0:T(8,128)} custom-call(s32[4]{0:T(128)} %off_ref.3, f32[16,576,128]{2,1,0:T(8,128)} %get-tuple-element.27.r_ref), custom_call_target="tpu_custom_call" | custom-call | tf_op jit(solution)/shard_map/finish/pallas_call | solution.py:228
Async XLA Ops:
  0.0 6.3 %collective-permute-start = (s32[1,16]{1,0:T(1,128)}, s32[1,16]{1,0:T(1,128)S(1)}, u32[]{:S(2)}, u32[]{:S(2)}) collective-permute-start(s32[1,16]{1,0:T(1,128)} %bitcast.25), channel_id=1, source_target_pairs={{0,1},{1,2},{2,3},{3,0},{4,5},{5,6},{6,7},{7,4},{8,9},{9,10},{10,1... | collective-permute-start | bytes 200 | tf_op jit(solution)/shard_map/ppermute | solution.py:327
  6.9 3.7 %collective-permute-start.1 = (s32[2,16]{1,0:T(2,128)S(1)}, s32[2,16]{1,0:T(2,128)S(1)}, u32[]{:S(2)}, u32[]{:S(2)}) collective-permute-start(s32[2,16]{1,0:T(2,128)S(1)} %pad_add_fusion.2), channel_id=1, source_target_pairs={{0,4},{4,8},{8,12},{12,0},{1,5},{5,9},{9,13},{13,1},{2,6},{6,10},{... | collective-permute-start | bytes 392 | tf_op jit(solution)/shard_map/ppermute | solution.py:327
  11.3 14.6 %copy-start = (s32[1,1,1,16]{3,2,1,0:T(1,128)S(1)}, s32[1,1,1,16]{3,2,1,0:T(1,128)}, u32[]{:S(2)}) copy-start(s32[1,1,1,16]{3,2,1,0:T(1,128)} %param.14) | copy-start | bytes 196
  11.3 14.6 %collective-permute-start.2 = (s32[4,16]{1,0:T(4,128)S(1)}, s32[4,16]{1,0:T(4,128)S(1)}, u32[]{:S(2)}, u32[]{:S(2)}) collective-permute-start(s32[4,16]{1,0:T(4,128)S(1)} %pad_add_fusion.1), channel_id=1, source_target_pairs={{0,16},{16,32},{32,48},{48,64},{64,80},{80,96},{96,112},{112,128},... | collective-permute-start | bytes 776 | tf_op jit(solution)/shard_map/ppermute | solution.py:327

commit v2 on v1

--- a/solution.py
+++ b/solution.py
@@ -25,58 +25,6 @@
         out[first] = jnp.where(low, a, pltpu.roll(b, distance, 1))
         out[second] = jnp.where(low, pltpu.roll(a, 128 - distance, 1), b)
     return out
-
-
-def pack_kernel(off_ref, slot_ref, x_ref, s_ref, tiles, place):
-    cell_z, cell_y = pl.program_id(0), pl.program_id(1)
-    ot, oz, oy, ox = off_ref[0], off_ref[1], off_ref[2], off_ref[3]
-
-    @pl.when((cell_z == 0) & (cell_y == 0))
-    def _():
-        def fill(i, _):
-            place[i // 16, slot_ref[i // 16, i % 16]] = i % 16
-            return 0
-        lax.fori_loop(0, 128, fill, 0)
-
-    lanes = lax.broadcasted_iota(jnp.int32, (12, 128), 1)
-    inside = (lanes & 63) < 64 - ox
-    for vb in range(3):
-        arrays = []
-        for t in range(4):
-            for m in range(4):
-                row = x_ref[(t + ot) & 3, 0, 0, 4 * vb + m]
-                turned = pltpu.roll(row, 128 - ox, 1)
-                arrays.append(jnp.where(inside, turned, pltpu.roll(turned, 64, 1)))
-        for bit in range(4):
-            arrays = swap_bits(arrays, bit, 4 << bit)
-        for j in range(16):
-            for part in range(3):
-                tiles[j, 3 * vb + part] = arrays[j][4 * part:4 * part + 4]
-    home = 2 * (cell_z >= 4 - oz).astype(jnp.int32) + (cell_y >= 4 - oy).astype(jnp.int32)
-    lane3 = lax.broadcasted_iota(jnp.int32, (9, 4, 128), 2)
-    mine = ((lane3 >> 4) & 3) < 4 - ot
-    def emit(q, _):
-        s_ref[q, 0, 0] = jnp.where(mine, tiles[place[home, q]], tiles[place[4 + home, q]])
-        return 0
-    lax.fori_loop(0, 16, emit, 0)
-
-
-def pack(offsets, slots, x):
-    def at(z, y, off, slot):
-        return (0, (z + off[1]) & 3, (y + off[2]) & 3, 0, 0, 0)
-    return pl.pallas_call(
-        pack_kernel,
-        out_shape=jax.ShapeDtypeStruct((16, 4, 4, 9, 4, 128), jnp.float32),
-        grid_spec=pltpu.PrefetchScalarGridSpec(
-            num_scalar_prefetch=2,
-            grid=(4, 4),
-            in_specs=[pl.BlockSpec((4, 1, 1, 12, 12, 128), at)],
-            out_specs=pl.BlockSpec((16, 1, 1, 9, 4, 128), lambda z, y, off, slot: (0, z, y, 0, 0, 0)),
-            scratch_shapes=[pltpu.VMEM((16, 9, 4, 128), jnp.float32), pltpu.SMEM((8, 16), jnp.int32)],
-        ),
-        compiler_params=pltpu.CompilerParams(dimension_semantics=("arbitrary", "arbitrary")),
-        name="pack",
-    )(offsets, slots, x)
 
 
 def cmul_sub(ar, ai, br, bi, cr, ci):
@@ -134,6 +82,7 @@
     ot = off_ref[0]
     lanes = lax.broadcasted_iota(jnp.int32, (12, 128), 1)
     mine = ((lanes >> 4) & 3) < 4 - ot
+    turn = (lanes & 124) | ((lanes + off_ref[3]) & 3)
 
     def unpack(n, _):
         after = (n + 1) & 15
@@ -145,6 +94,7 @@
             for bit in range(4):
                 arrays = swap_bits(arrays, bit, 4 << bit)
             arrays = swap_bits(arrays, 2, 64)
+            arrays = [jnp.take_along_axis(array, turn, axis=1, mode="promise_in_bounds") for array in arrays]
             for at in range(16):
                 thi, ri, m = at >> 3, (at >> 2) & 1, at & 3
                 sites[n, thi, pl.ds(ri * 12 + 4 * vb + m, 12, stride=24)] = arrays[at]
@@ -241,20 +191,17 @@
     return out.transpose(0, 1, 2, 3, 5, 4, 6).reshape(16, 2, 12, 6, 2, 256)
 
 
-WAYS = ((1, 1), (1, 0), (0, 1), (0, 0))
-
-
-def exchange_kernel(oz, oy, s_ref, r_ref, send, recv, local):
+def exchange_kernel(oz, oy, off_ref, place_ref, x_ref, r_ref, tiles, s_ref, send, recv, local):
     a, b, c = lax.axis_index("ta"), lax.axis_index("gz"), lax.axis_index("gy")
     n_a, n_b, n_c = lax.axis_size("ta"), lax.axis_size("gz"), lax.axis_size("gy")
-    spans_z = ((0, 4 - oz), (4 - oz, oz))
-    spans_y = ((0, 4 - oy), (4 - oy, oy))
+    ot, ox = off_ref[0], off_ref[3]
+    spans = ((0, 4 - oy), (4 - oy, oy))
 
     barrier = pltpu.get_barrier_semaphore()
 
     def greet(step, _):
         q = lax.rem(a + step, n_a)
-        for dz, dy in WAYS[:3]:
+        for dz, dy in ((1, 1), (1, 0), (0, 1)):
             peer = (q, lax.rem(b + dz, n_b), lax.rem(c + dy, n_c))
             pl.semaphore_signal(barrier, inc=1, device_id=peer, device_id_type=MESH)
 
@@ -265,75 +212,161 @@
         return 0
 
     lax.fori_loop(1, n_a + 1, greet, 0)
-    pl.semaphore_wait(barrier, 4 * n_a - 1)
-
-    def view(ref, at, dz, dy):
-        z0, nz = spans_z[dz]
-        y0, ny = spans_y[dy]
-        return ref.at[at, pl.ds(z0, nz), pl.ds(y0, ny)]
-
-    def copy(way, q, lands):
-        dz, dy = WAYS[way]
+
+    lanes = lax.broadcasted_iota(jnp.int32, (8, 128), 1)
+    stays = (lanes & 3) >= ox
+    lanes4 = lax.broadcasted_iota(jnp.int32, (4, 128), 1)
+    mine = ((lanes4 >> 4) & 3) < 4 - ot
+
+    def copy(z, dz, dy, q, lands):
+        y0, ny = spans[dy]
         return pltpu.make_async_remote_copy(
-            view(s_ref, q, dz, dy),
-            view(r_ref, lands, dz, dy),
-            send.at[way, q],
-            recv.at[way, lands],
+            s_ref.at[q, z, pl.ds(y0, ny)],
+            r_ref.at[lands, z, pl.ds(y0, ny)],
+            send.at[z, dy, q],
+            recv.at[z, dy, lands],
             device_id=(q, lax.rem(b + n_b - dz, n_b), lax.rem(c + n_c - dy, n_c)),
             device_id_type=MESH,
         )
 
-    def start(step, _):
-        q = lax.rem(a + step, n_a)
-        for way in range(3):
-            copy(way, q, a).start()
-        pl.when(step < n_a)(copy(3, q, a).start)
-        return 0
-
-    own = pltpu.make_async_copy(view(s_ref, a, 0, 0), view(r_ref, a, 0, 0), local)
-    lax.fori_loop(1, n_a + 1, start, 0)
-    own.start()
-
-    def finish_one(way, q):
-        one = copy(way, q, q)
+    def own(z):
+        y0, ny = spans[0]
+        return pltpu.make_async_copy(s_ref.at[a, z, pl.ds(y0, ny)], r_ref.at[a, z, pl.ds(y0, ny)], local.at[z])
+
+    def plane(z, dz):
+        from_z = lax.rem(z + oz, 4)
+
+        def spread(step, _):
+            vb, part = step // 6, lax.rem(step, 6)
+            rows = pl.ds(pl.multiple_of(8 * part, 8), 8)
+            arrays = [x_ref[(t + ot) & 3, from_z, 4 * vb + m, rows] for t in range(4) for m in range(4)]
+            for bit in range(4):
+                arrays = swap_bits(arrays, bit, 4 << bit)
+            for j in range(16):
+                row = pl.multiple_of(j * 144 + vb * 48 + 8 * part, 8)
+                tiles[pl.ds(row, 8)] = jnp.where(stays, arrays[j], arrays[(j + 1) % 16])
+            return 0
+
+        lax.fori_loop(0, 18, spread, 0)
+
+        def emit(q, _):
+            for y in range(4):
+                home = 2 * dz + (y >= 4 - oy)
+                first = place_ref[home, q] * 144 + (y + oy) % 4
+                second = place_ref[4 + home, q] * 144 + (y + oy) % 4
+                for g in range(9):
+                    s_ref[q, z, y, g] = jnp.where(
+                        mine,
+                        tiles[pl.ds(first + 16 * g, 4, stride=4)],
+                        tiles[pl.ds(second + 16 * g, 4, stride=4)],
+                    )
+            return 0
+
+        lax.fori_loop(0, 16, emit, 0)
+
+    def start(z, dz):
+        def one(step, _):
+            q = lax.rem(a + step, n_a)
+            copy(z, dz, 1, q, a).start()
+            if dz:
+                copy(z, dz, 0, q, a).start()
+            else:
+                pl.when(step < n_a)(copy(z, dz, 0, q, a).start)
+            return 0
+
+        lax.fori_loop(1, n_a + 1, one, 0)
+        if not dz:
+            own(z).start()
+
+    def finish_one(z, dz, dy, q):
+        one = copy(z, dz, dy, q, q)
         one.wait_send()
         one.wait_recv()
 
-    def wait(step, _):
-        q = lax.rem(a + step, n_a)
-        for way in range(3):
-            finish_one(way, q)
-        pl.when(step < n_a)(functools.partial(finish_one, 3, q))
-        return 0
-
-    lax.fori_loop(1, n_a + 1, wait, 0)
-    own.wait()
-
-
-def exchange(s, oz, oy):
+    def wait(z, dz):
+        def one(step, _):
+            q = lax.rem(a + step, n_a)
+            finish_one(z, dz, 1, q)
+            if dz:
+                finish_one(z, dz, 0, q)
+            else:
+                pl.when(step < n_a)(functools.partial(finish_one, z, dz, 0, q))
+            return 0
+
+        lax.fori_loop(1, n_a + 1, one, 0)
+        if not dz:
+            own(z).wait()
+
+    def both(dz, first, last):
+        def run(z, _):
+            plane(z, dz)
+
+            @pl.when(z == ORDER_FIRST[oz])
+            def _():
+                pl.semaphore_wait(barrier, 4 * n_a - 1)
+
+            start(z, dz)
+            return 0
+
+        lax.fori_loop(first, last, run, 0)
+
+    both(1, 4 - oz, 4)
+    both(0, 0, 4 - oz)
+
+    for dz, first, last in ((1, 4 - oz, 4), (0, 0, 4 - oz)):
+        def done(z, _):
+            wait(z, dz)
+            return 0
+
+        lax.fori_loop(first, last, done, 0)
+
+
+ORDER_FIRST = {1: 3, 2: 2, 3: 1}
+
+
+def exchange(offsets, place, x, oz, oy):
     return pl.pallas_call(
         functools.partial(exchange_kernel, oz, oy),
-        out_shape=jax.ShapeDtypeStruct(s.shape, s.dtype),
-        in_specs=[pl.BlockSpec(memory_space=pl.ANY)],
+        out_shape=jax.ShapeDtypeStruct((16, 4, 4, 9, 4, 128), jnp.float32),
+        in_specs=[
+            pl.BlockSpec(memory_space=pltpu.SMEM),
+            pl.BlockSpec(memory_space=pltpu.SMEM),
+            pl.BlockSpec(memory_space=pltpu.VMEM),
+        ],
         out_specs=pl.BlockSpec(memory_space=pl.ANY),
-        scratch_shapes=[pltpu.SemaphoreType.DMA((4, 16)), pltpu.SemaphoreType.DMA((4, 16)), pltpu.SemaphoreType.DMA],
+        scratch_shapes=[
+            pltpu.VMEM((16 * 144, 128), jnp.float32),
+            pltpu.VMEM((16, 4, 4, 9, 4, 128), jnp.float32),
+            pltpu.SemaphoreType.DMA((4, 2, 16)),
+            pltpu.SemaphoreType.DMA((4, 2, 16)),
+            pltpu.SemaphoreType.DMA((4,)),
+        ],
         compiler_params=pltpu.CompilerParams(has_side_effects=True, collective_id=3 * (oz - 1) + oy - 1),
         name=f"exchange_{oz}{oy}",
-    )(s)
-
-
-def ahead(array, axis):
-    length = lax.axis_size(axis)
-    return lax.ppermute(array, axis, [(i, (i + 1) % length) for i in range(length)])
+    )(offsets, place, x)
+
+
+def slots_of_homes(slots):
+    names = ("ta", "gz", "gy")
+    sizes = [lax.axis_size(name) for name in names]
+    ranks = [(i, j, k) for i in range(sizes[0]) for j in range(sizes[1]) for k in range(sizes[2])]
+    number = {rank: n for n, rank in enumerate(ranks)}
+    rows = [slots]
+    for code in range(1, 8):
+        by = ((code >> 2) & 1, (code >> 1) & 1, code & 1)
+        pairs = [(n, number[tuple((r + d) % size for r, d, size in zip(rank, by, sizes))]) for n, rank in enumerate(ranks)]
+        rows.append(lax.ppermute(slots, names, pairs))
+    return jnp.concatenate(rows, axis=0)
 
 
 def per_device(near_null, offsets, owner_slot):
-    slots = owner_slot.reshape(1, 16)
-    for axis in ("gy", "gz", "ta"):
-        slots = jnp.concatenate([slots, ahead(slots, axis)], axis=0)
-    s = pack(offsets, slots, near_null)
+    slots = slots_of_homes(owner_slot.reshape(1, 16))
+    spots = jnp.arange(16, dtype=jnp.int32)
+    hits = slots[:, :, None] == spots[None, None, :]
+    place = jnp.sum(jnp.where(hits, spots[None, :, None], 0), axis=1)
+    x = near_null.transpose(0, 1, 3, 4, 2, 5).reshape(4, 4, 12, 48, 128)
     branches = [functools.partial(exchange, oz=oz, oy=oy) for oz in (1, 2, 3) for oy in (1, 2, 3)]
-    r = lax.switch(3 * (offsets[1] - 1) + offsets[2] - 1, branches, s)
+    r = lax.switch(3 * (offsets[1] - 1) + offsets[2] - 1, branches, offsets, place, x)
     return finish(offsets, r)
 
 

time: 244 us -> 224 us (0.918); the launches traced: 244 us -> 227 us
  Pallas kernels: 217 us -> 203 us
  local copies, waits for them, and re-layouts: 7.25 us -> 2.05 us
  starting transfers between devices: 12.5 us -> 16 us
    pallas_call x1 -> x0, Pallas kernels: 40.7 us -> none  [pack(): pl.pallas_call(pack_kernel, out_shape=jax.ShapeDtypeStruct((16, 4, 4, 9,...]
    pallas_call x1, Pallas kernels: 130 us -> 153 us  [exchange(): pl.pallas_call(functools.partial(exchange_kernel, oz, oy), out_shape=jax....]
    unnamed x3 -> x0, local copies, waits for them, and re-layouts: 5.94 us -> none
    ppermute x3 -> x7, starting transfers between devices: 12.5 us -> 16 us  [slots_of_homes(): rows.append(lax.ppermute(slots, names, pairs))]
    pallas_call x1, Pallas kernels: 46.9 us -> 49.9 us  [finish(): pl.pallas_call(finish_kernel, out_shape=jax.ShapeDtypeStruct((9216, 128),...]
  transfers between devices with their start and end apart: 3 -> 7, of which waited for: 2 -> 3; matrix products, arithmetic and copies ran while one was open for 3% -> 1% of each run, Pallas kernels for 0% -> 0%
where the time goes in v2:
time: 224 us; the launch traced here: 227 us
  Pallas kernels  203 us (91%)
  starting transfers between devices  16 us (7%)
  waiting for transfers between devices  3.89 us (2%)
    pallas_call x1, Pallas kernels, exchange(): pl.pallas_call(functools.partial(exchange_kernel, oz, oy), out_shape=jax....  153 us
    pallas_call x1, Pallas kernels, finish(): pl.pallas_call(finish_kernel, out_shape=jax.ShapeDtypeStruct((9216, 128),...  49.9 us
    ppermute x7, starting transfers between devices, slots_of_homes(): rows.append(lax.ppermute(slots, names, pairs))  16 us
  transfers between devices with their start and end apart: 7, of which 3 were waited for; matrix products, arithmetic and copies ran while one was open for 1% of the time, Pallas kernels for 0%

profile of v2, /device:TPU:1, one launch (start us, length us, event | category | flops | bytes accessed | tf_op | source)
XLA Modules:
  0.0 226.5 jit_solution(15716733266300585409)
XLA Ops:
  0.0 8.9 %collective-permute-start.6 = (s32[1,16]{1,0:T(1,128)}, s32[1,16]{1,0:T(1,128)S(1)}, u32[]{:S(2)}, u32[]{:S(2)}) collective-permute-start(s32[1,16]{1,0:T(1,128)} %bitcast.37), channel_id=1, source_target_pairs={{0,21},{1,22},{2,23},{3,20},{4,25},{5,26},{6,27},{7,24},{8,29},{9,... | collective-permute-start | bytes 200 | tf_op jit(solution)/shard_map/ppermute | solution.py:358
  8.9 1.9 collective-permute-start.5
  10.8 0.4 collective-permute-start.4
  11.2 1.8 collective-permute-start.3
  13.0 2.4 %collective-permute-start.2 = (s32[1,16]{1,0:T(1,128)}, s32[1,16]{1,0:T(1,128)S(1)}, u32[]{:S(2)}, u32[]{:S(2)}) collective-permute-start(s32[1,16]{1,0:T(1,128)} %bitcast.41), channel_id=1, source_target_pairs={{0,5},{1,6},{2,7},{3,4},{4,9},{5,10},{6,11},{7,8},{8,13},{9,14},{1... | collective-permute-start | bytes 200 | tf_op jit(solution)/shard_map/ppermute | solution.py:358
  15.3 1.4 fusion
  18.0 0.0 collective-permute-done.6
  18.0 0.1 collective-permute-start.1
  18.1 0.0 collective-permute-done.5
  18.1 0.5 collective-permute-start
  18.7 0.0 collective-permute-done.4
  18.7 0.0 collective-permute-done.3
  18.7 0.8 collective-permute-done.2
  19.4 2.4 %collective-permute-done.1 = s32[1,16]{1,0:T(1,128)S(1)} collective-permute-done((s32[1,16]{1,0:T(1,128)}, s32[1,16]{1,0:T(1,128)S(1)}, u32[]{:S(2)}, u32[]{:S(2)}) %collective-permute-start.1) | collective-permute-done | bytes 96 | tf_op jit(solution)/shard_map/ppermute | solution.py:358
  21.8 0.7 collective-permute-done
  22.5 0.7 concatenate.3
  23.2 0.1 select_reduce_fusion
  23.3 153.3 %conditional.1 = (f32[16,576,128]{2,1,0:T(8,128)}) conditional(s32[]{:T(128)} %bitcast.9, (s32[4]{0:T(128)}, s32[8,16]{1,0:T(8,128)S(1)}, f32[4,4,12,48,128]{4,3,2,1,0:T(8,128)}) %tuple.52, (s32[4]{0:T(128)}, s32[8,16]{1,0:T(8,128)S(1)}, f32[4,4,12,48,128]{4,3,2,1,0:T(8,128)}) %tuple.53, (s32[4]{0:T(128)}, ...), branch_computations={%region_1.2_spmd, %region_2.3_spmd, %region_3.4_spmd, %region_4.5_... | conditional | bytes 8 | solution.py:369
  23.3 153.0 %exchange_13.1 = f32[16,4,4,9,4,128]{5,4,3,2,1,0:T(4,128)} custom-call(s32[4]{0:T(128)} %get-tuple-element.76.off_ref, s32[8,16]{1,0:T(8,128)S(1)} %get-tuple-element.77.place_ref, f32[4,4,12,48,128]{4,3,2,1,0:T(8,128)} %get-tuple-element.78.x_ref), custom_call_target="tpu_custom_call" | custom-call | tf_op jit(solution)/shard_map/cond/branch_2_fun/exchange_13/pallas_call | solution.py:328
  176.6 49.9 %finish.1 = f32[9216,128]{1,0:T(8,128)} custom-call(s32[4]{0:T(128)} %off_ref.1, f32[16,576,128]{2,1,0:T(8,128)} %get-tuple-element.99.r_ref), custom_call_target="tpu_custom_call" | custom-call | tf_op jit(solution)/shard_map/finish/pallas_call | solution.py:178
Async XLA Ops:
  0.0 18.0 %collective-permute-start.6 = (s32[1,16]{1,0:T(1,128)}, s32[1,16]{1,0:T(1,128)S(1)}, u32[]{:S(2)}, u32[]{:S(2)}) collective-permute-start(s32[1,16]{1,0:T(1,128)} %bitcast.37), channel_id=1, source_target_pairs={{0,21},{1,22},{2,23},{3,20},{4,25},{5,26},{6,27},{7,24},{8,29},{9,... | collective-permute-start | bytes 200 | tf_op jit(solution)/shard_map/ppermute | solution.py:358
  8.9 9.2 %collective-permute-start.5 = (s32[1,16]{1,0:T(1,128)}, s32[1,16]{1,0:T(1,128)S(1)}, u32[]{:S(2)}, u32[]{:S(2)}) collective-permute-start(s32[1,16]{1,0:T(1,128)} %bitcast.38), channel_id=1, source_target_pairs={{0,20},{1,21},{2,22},{3,23},{4,24},{5,25},{6,26},{7,27},{8,28},{9,... | collective-permute-start | bytes 200 | tf_op jit(solution)/shard_map/ppermute | solution.py:358
  10.8 7.9 %collective-permute-start.4 = (s32[1,16]{1,0:T(1,128)}, s32[1,16]{1,0:T(1,128)S(1)}, u32[]{:S(2)}, u32[]{:S(2)}) collective-permute-start(s32[1,16]{1,0:T(1,128)} %bitcast.39), channel_id=1, source_target_pairs={{0,17},{1,18},{2,19},{3,16},{4,21},{5,22},{6,23},{7,20},{8,25},{9,... | collective-permute-start | bytes 200 | tf_op jit(solution)/shard_map/ppermute | solution.py:358
  11.2 7.5 %collective-permute-start.3 = (s32[1,16]{1,0:T(1,128)}, s32[1,16]{1,0:T(1,128)S(1)}, u32[]{:S(2)}, u32[]{:S(2)}) collective-permute-start(s32[1,16]{1,0:T(1,128)} %bitcast.40), channel_id=1, source_target_pairs={{0,16},{1,17},{2,18},{3,19},{4,20},{5,21},{6,22},{7,23},{8,24},{9,... | collective-permute-start | bytes 200 | tf_op jit(solution)/shard_map/ppermute | solution.py:358
  13.0 6.5 %collective-permute-start.2 = (s32[1,16]{1,0:T(1,128)}, s32[1,16]{1,0:T(1,128)S(1)}, u32[]{:S(2)}, u32[]{:S(2)}) collective-permute-start(s32[1,16]{1,0:T(1,128)} %bitcast.41), channel_id=1, source_target_pairs={{0,5},{1,6},{2,7},{3,4},{4,9},{5,10},{6,11},{7,8},{8,13},{9,14},{1... | collective-permute-start | bytes 200 | tf_op jit(solution)/shard_map/ppermute | solution.py:358
  18.0 3.8 %collective-permute-start.1 = (s32[1,16]{1,0:T(1,128)}, s32[1,16]{1,0:T(1,128)S(1)}, u32[]{:S(2)}, u32[]{:S(2)}) collective-permute-start(s32[1,16]{1,0:T(1,128)} %bitcast.42), channel_id=1, source_target_pairs={{0,4},{1,5},{2,6},{3,7},{4,8},{5,9},{6,10},{7,11},{8,12},{9,13},{1... | collective-permute-start | bytes 200 | tf_op jit(solution)/shard_map/ppermute | solution.py:358
  18.1 4.4 %collective-permute-start = (s32[1,16]{1,0:T(1,128)}, s32[1,16]{1,0:T(1,128)S(1)}, u32[]{:S(2)}, u32[]{:S(2)}) collective-permute-start(s32[1,16]{1,0:T(1,128)} %bitcast.43), channel_id=1, source_target_pairs={{0,1},{1,2},{2,3},{3,0},{4,5},{5,6},{6,7},{7,4},{8,9},{9,10},{10,1... | collective-permute-start | bytes 200 | tf_op jit(solution)/shard_map/ppermute | solution.py:358
